TPU v7x, 256 devices: a whole 4x4x8 slice. The times are simulated.
256 devices in a mesh: rows: 8 (over z), centers: 32 (over y, x, core).
Axes of the slice: x: 4, y: 4, z: 8, core: 2. Of those that a mesh axis runs over, the one named last changes fastest.
Arguments:
- features: float32 [8192, 128], P('rows'), may hold values from -6 to 6
- centers: float32 [16384, 128], P('centers'), may hold values from -6 to 6
- labels: int32 [8192, 64], P('rows'), may hold values 0 or 1
- coeffs: float32 [16384, 64], P('centers'), may hold values from -3 to 3
- precond: float32 [16384, 16384], P('rows', 'centers'), may hold values from -2 to 2, as said below
Outputs:
- coeffs_out: float32 [16384, 64], P('centers')
Inputs may be any that keep to these rules, and one draw needn't show every extreme that they name: precond is lower triangular: every entry above the diagonal is zero, and its diagonal is positive.
All inputs are finite; a program needn't handle non-finite values. No bound on the sum of `labels` on one device may be relied on, other than what follows from the above.
Results may differ from a plain program's by a relative error of at most 0.0003.
Values sent between devices are 32-bit elements; how exact they have to be, the bound alone decides.
A program may use at most 64 MiB of HBM per device.

v0:
```python
import functools

import jax
import jax.numpy as jnp
from jax import lax
from jax.experimental import pallas as pl
from jax.experimental.pallas import tpu as pltpu
from jax.sharding import PartitionSpec as P

STEPS = 2
step_size = 0.5
epsilon = 1e-06

Z, Y, X = 8, 4, 4
CHIPS = Y * X
D = 128
OUT = 64
OUTS = OUT // 2
GROUPS = OUTS // 8
ROWS = 1024
CENT = 512
PROWS = 2048
RS_ROWS = ROWS // X
RS_PROWS = PROWS // X
FAR_FIRST = (2, 1, 3, 0)
Z_EVEN = (4, 2, 6)
Z_ODD = (3, 5, 1, 7)
f32 = jnp.float32
bf16 = jnp.bfloat16
MESH = pl.DeviceIdType.MESH


def split(x):
    hi = x.astype(bf16)
    lo = (x - hi.astype(f32)).astype(bf16)
    return hi, lo


def stacked(x):
    hi, lo = split(x)
    return jnp.concatenate([hi, lo], axis=0), hi


def product(lhs, w_hi, w_lo, contract):
    both, hi = lhs
    dims = (((1,), (contract,)), ((), ()))
    r = lax.dot_general(both, w_hi, dims, preferred_element_type=f32)
    s = lax.dot_general(hi, w_lo, dims, preferred_element_type=f32)
    return r[:OUTS] + r[OUTS:] + s


def kernel(
    feat_hbm, cent_hbm, lab_hbm, coef_hbm, prec_hbm, out_ref,
    feat, cent, lab, labt, coef, coeft, k_hi, k_lo, p_raw, p_hi, p_lo,
    log_p, log_r, res_f, gra_p, gra_r, gra_f, fwd_p, fwd_r, fwd_f, bak_p, bak_r, a_f, sq_s, sq_r, fin_s, fin_r,
    load_sem, pair_send, pair_recv,
    log_ss, log_rs, res_ss, res_rs, gra_ss, gra_rs, grf_ss, grf_rs,
    fwd_ss, fwd_rs, fwf_ss, fwf_rs, bak_ss, bak_rs, af_ss, af_rs,
):
    z = lax.axis_index("rows")
    c = lax.axis_index("centers")
    j = c // 2
    k = c % 2
    y = j // X
    x = j % X
    zlo = z % 2
    partner = c + 1 - 2 * k
    my_rg = x

    lab_row = pl.multiple_of(x * RS_ROWS, RS_ROWS)
    loads = [
        pltpu.make_async_copy(feat_hbm, feat, load_sem.at[0]),
        pltpu.make_async_copy(cent_hbm, cent.at[k], load_sem.at[1]),
        pltpu.make_async_copy(coef_hbm, coef.at[k], load_sem.at[2]),
        pltpu.make_async_copy(lab_hbm.at[pl.ds(lab_row, RS_ROWS), :], lab, load_sem.at[3]),
        pltpu.make_async_copy(prec_hbm, p_raw.at[k], load_sem.at[4]),
    ]
    for copy in loads:
        copy.start()

    barrier = pltpu.get_barrier_semaphore()
    pl.semaphore_signal(barrier, inc=1, device_id=(z, partner), device_id_type=MESH)

    def chip_at(dy, dx):
        return lax.rem(y + dy, Y) * X + lax.rem(x + dx, X)

    plane = [(dy, dx) for dx in FAR_FIRST for dy in FAR_FIRST if (dy, dx) != (0, 0)]
    for dy, dx in plane:
        pl.semaphore_signal(barrier, inc=1, device_id=(z, 2 * chip_at(dy, dx) + k), device_id_type=MESH)
    for oz in Z_EVEN + Z_ODD:
        pl.semaphore_signal(barrier, inc=1, device_id=(lax.rem(z + oz, Z), c), device_id_type=MESH)

    def remote(src, dst, send, recv, device):
        return pltpu.make_async_remote_copy(
            src_ref=src, dst_ref=dst, send_sem=send, recv_sem=recv, device_id=device, device_id_type=MESH
        )

    def to_plane(src, dst, ss, rs, dy, dx):
        o = dy * X + dx
        return remote(src, dst, ss.at[o], rs.at[o], (z, 2 * chip_at(dy, dx) + k))

    def to_z(src, dst, ss, rs, oz):
        return remote(src, dst, ss.at[oz], rs.at[oz], (lax.rem(z + oz, Z), c))

    loads[0].wait()
    loads[1].wait()
    fx = feat[...]
    row_norm = lax.dot_general(
        jnp.ones((8, D), f32), fx * fx, (((1,), (1,)), ((), ())),
        precision=lax.Precision.HIGHEST, preferred_element_type=f32,
    )[:1]

    def kernel_half(h):
        @pl.loop(0, CENT // 128)
        def _(i):
            at = pl.multiple_of(i * 128, 128)
            cx = cent[h, pl.ds(at, 128), :]
            cn = jnp.sum(cx * cx, axis=1, keepdims=True)
            cross = lax.dot_general(
                cx, feat[...], (((1,), (1,)), ((), ())),
                precision=lax.Precision.HIGHEST, preferred_element_type=f32,
            )
            tile = jnp.exp(-2.0 * (cn + row_norm - 2.0 * cross) / D)
            hi, lo = split(tile)
            k_hi[h, pl.ds(at, 128), :] = hi
            k_lo[h, pl.ds(at, 128), :] = lo

    kernel_half(k)
    loads[2].wait()
    coeft[k] = coef[k].T

    pl.semaphore_wait(barrier, 1 + len(plane) + Z - 1)
    cent_pair = remote(cent_hbm, cent.at[k], pair_send.at[0], pair_recv.at[0], (z, partner))
    coef_pair = remote(coef_hbm, coef.at[k], pair_send.at[1], pair_recv.at[1], (z, partner))
    prec_pair = remote(prec_hbm, p_raw.at[k], pair_send.at[2], pair_recv.at[2], (z, partner))
    cent_pair.start()
    coef_pair.start()
    prec_pair.start()
    other = 1 - k
    loads[3].wait()
    labt[...] = lab[...].astype(f32).T
    cent_pair.wait()
    kernel_half(other)
    coef_pair.wait()
    coeft[other] = coef[other].T
    for og in range(GROUPS):
        at = pl.multiple_of(k * OUTS + og * 8, 8)
        for h in range(2):
            a_f[og * 2 + h] = coeft[h, pl.ds(at, 8), :]
    targets = labt[pl.ds(pl.multiple_of(k * OUTS + y * 8, 8), 8), :]

    def half_of(pieces, h):
        return jnp.concatenate([pieces[og * 2 + h] for og in range(GROUPS)], axis=0)

    def line_of(pieces):
        return jnp.concatenate(
            [
                jnp.concatenate([pieces[og * X + rg] for rg in range(X)], axis=1)
                for og in range(GROUPS)
            ],
            axis=0,
        )

    def precond_half(h):
        @pl.loop(0, PROWS // 128)
        def _(i):
            at = pl.multiple_of(i * 128, 128)
            hi, lo = split(p_raw[h, pl.ds(at, 128), :])
            p_hi[h, pl.ds(at, 128), :] = hi
            p_lo[h, pl.ds(at, 128), :] = lo

    for step in range(STEPS):
        lhs = [stacked(half_of(a_f, h)) for h in range(2)]
        sends = []
        for dx in FAR_FIRST:
            rg = lax.rem(x + dx, X)
            at = pl.ds(pl.multiple_of(rg * RS_ROWS, RS_ROWS), RS_ROWS)
            part = product(lhs[0], k_hi[0, :, at], k_lo[0, :, at], 0) + product(
                lhs[1], k_hi[1, :, at], k_lo[1, :, at], 0
            )
            for og in range(GROUPS):
                log_p[og * X + rg] = part[og * 8 : og * 8 + 8]
            for dy in FAR_FIRST:
                if (dy, dx) != (0, 0):
                    copy = to_plane(log_p.at[chip_at(dy, dx)], log_r.at[dy * X + dx], log_ss, log_rs, dy, dx)
                    copy.start()
                    sends.append(copy)
        if step == 0:
            loads[4].wait()
            precond_half(k)
        total = log_p[j]
        for copy, (dy, dx) in reversed(list(zip(sends, plane))):
            copy.wait_recv()
            total = total + log_r[dy * X + dx]
        res_f[j] = (jax.nn.sigmoid(total) - targets) * (1.0 / (ROWS * Z))

        gathers = []
        for dy, dx in plane:
            copy = to_plane(res_f.at[j], res_f.at[j], res_ss, res_rs, dy, dx)
            copy.start()
            gathers.append(copy)
        if step == 0:
            prec_pair.wait()
            precond_half(other)
        for copy in sends:
            copy.wait_send()
        for copy in reversed(gathers):
            copy.wait_recv()
        lhs = stacked(line_of(res_f))
        for copy in gathers:
            copy.wait_send()

        sends = []
        for rel, offsets in ((0, Z_EVEN), (1, Z_ODD)):
            cg = lax.rem(zlo + rel, 2)
            for s in range(2):
                at = slice(s * 256, s * 256 + 256)
                part = product(lhs, k_hi[cg, at, :], k_lo[cg, at, :], 1)
                for og in range(GROUPS):
                    gra_p[og * 2 + cg, :, at] = part[og * 8 : og * 8 + 8]
            for oz in offsets:
                copy = to_z(gra_p.at[lax.rem(z + oz, Z)], gra_r.at[oz], gra_ss, gra_rs, oz)
                copy.start()
                sends.append((oz, copy))
        total = gra_p[z]
        for oz, copy in reversed(sends):
            copy.wait_recv()
            total = total + gra_r[oz]
        gra_f[z] = total
        gathers = []
        for oz in Z_EVEN + Z_ODD:
            copy = to_z(gra_f.at[z], gra_f.at[z], grf_ss, grf_rs, oz)
            copy.start()
            gathers.append(copy)
        for oz, copy in sends:
            copy.wait_send()
        for copy in reversed(gathers):
            copy.wait_recv()
        lhs = [stacked(half_of(gra_f, h)) for h in range(2)]
        for copy in gathers:
            copy.wait_send()

        sends = []
        for dx in FAR_FIRST:
            rg = lax.rem(x + dx, X)
            for s in range(2):
                at = pl.ds(pl.multiple_of(rg * RS_PROWS + s * 256, 256), 256)
                part = product(lhs[0], p_hi[0, at, :], p_lo[0, at, :], 1) + product(
                    lhs[1], p_hi[1, at, :], p_lo[1, at, :], 1
                )
                for og in range(GROUPS):
                    fwd_p[og * X + rg, :, s * 256 : s * 256 + 256] = part[og * 8 : og * 8 + 8]
            for dy in FAR_FIRST:
                if (dy, dx) != (0, 0):
                    copy = to_plane(fwd_p.at[chip_at(dy, dx)], fwd_r.at[dy * X + dx], fwd_ss, fwd_rs, dy, dx)
                    copy.start()
                    sends.append(copy)
        total = fwd_p[j]
        for copy, (dy, dx) in reversed(list(zip(sends, plane))):
            copy.wait_recv()
            total = total + fwd_r[dy * X + dx]
        fwd_f[j] = total
        gathers = []
        for dy, dx in plane:
            copy = to_plane(fwd_f.at[j], fwd_f.at[j], fwf_ss, fwf_rs, dy, dx)
            copy.start()
            gathers.append(copy)
        for copy in sends:
            copy.wait_send()
        for copy in reversed(gathers):
            copy.wait_recv()
        square = jnp.zeros((8, RS_PROWS), f32)
        for i in range(CHIPS):
            square = square + fwd_f[i] * fwd_f[i]
        square = square[:, :256] + square[:, 256:]
        square = square[:, :128] + square[:, 128:]
        sq_s[step] = square
        sq_pair = remote(
            sq_s.at[step], sq_r.at[step], pair_send.at[3 + step], pair_recv.at[3 + step], (z, partner)
        )
        sq_pair.start()
        lhs = stacked(line_of(fwd_f))
        for copy in gathers:
            copy.wait_send()

        def back_part(cg):
            for s in range(2):
                at = slice(s * 256, s * 256 + 256)
                part = product(lhs, p_hi[cg, :, at], p_lo[cg, :, at], 0)
                for og in range(GROUPS):
                    bak_p[og * 2 + cg, :, at] = part[og * 8 : og * 8 + 8]

        sends = []
        for rel, offsets in ((0, Z_EVEN), (1, Z_ODD)):
            cg = lax.rem(zlo + rel, 2)
            back_part(cg)
            if rel == 0:
                sq_pair.wait()
                square = square + sq_r[step]
                for i in range(Z):
                    bak_p[i, :, CENT:] = square
            for oz in offsets:
                copy = to_z(bak_p.at[lax.rem(z + oz, Z)], bak_r.at[oz], bak_ss, bak_rs, oz)
                copy.start()
                sends.append((oz, copy))
        total = bak_p[z]
        for oz, copy in reversed(sends):
            copy.wait_recv()
            total = total + bak_r[oz]
        squares = jnp.sum(jnp.sum(total[:, CENT:], axis=1, keepdims=True), axis=0, keepdims=True)
        scale = step_size / jnp.sqrt(squares / (CENT * 2 * CHIPS * OUT) + epsilon)
        a_f[z] = a_f[z] - scale * total[:, :CENT]
        gathers = []
        for oz in Z_EVEN + Z_ODD:
            copy = to_z(a_f.at[z], a_f.at[z], af_ss, af_rs, oz)
            copy.start()
            gathers.append(copy)
        for oz, copy in sends:
            copy.wait_send()
        for copy in reversed(gathers):
            copy.wait_recv()
        for copy in gathers:
            copy.wait_send()

    for og in range(GROUPS):
        fin_s[og] = a_f[og * 2 + other]
    fin_pair = remote(fin_s, fin_r, pair_send.at[5], pair_recv.at[5], (z, partner))
    fin_pair.start()
    mine = pl.multiple_of(k * OUTS, OUTS)
    theirs = pl.multiple_of(other * OUTS, OUTS)
    for og in range(GROUPS):
        out_ref[pl.ds(mine + og * 8, 8), :] = a_f[og * 2 + k]
    fin_pair.wait()
    for og in range(GROUPS):
        out_ref[pl.ds(theirs + og * 8, 8), :] = fin_r[og]


def body(features, centers, labels, coeffs, precond):
    any_space = pl.BlockSpec(memory_space=pl.ANY)
    V = pltpu.VMEM
    dma = pltpu.SemaphoreType.DMA
    scratch = [
        V((ROWS, D), f32),
        V((2, CENT, D), f32),
        V((RS_ROWS, OUT), jnp.int32),
        V((OUT, RS_ROWS), f32),
        V((2, CENT, OUT), f32),
        V((2, OUT, CENT), f32),
        V((2, CENT, ROWS), bf16),
        V((2, CENT, ROWS), bf16),
        V((2, PROWS, CENT), f32),
        V((2, PROWS, CENT), bf16),
        V((2, PROWS, CENT), bf16),
        V((CHIPS, 8, RS_ROWS), f32),
        V((CHIPS, 8, RS_ROWS), f32),
        V((CHIPS, 8, RS_ROWS), f32),
        V((Z, 8, CENT), f32),
        V((Z, 8, CENT), f32),
        V((Z, 8, CENT), f32),
        V((CHIPS, 8, RS_PROWS), f32),
        V((CHIPS, 8, RS_PROWS), f32),
        V((CHIPS, 8, RS_PROWS), f32),
        V((Z, 8, CENT + 128), f32),
        V((Z, 8, CENT + 128), f32),
        V((Z, 8, CENT), f32),
        V((STEPS, 8, 128), f32),
        V((STEPS, 8, 128), f32),
        V((GROUPS, 8, CENT), f32),
        V((GROUPS, 8, CENT), f32),
        dma((5,)),
        dma((6,)),
        dma((6,)),
    ]
    for count in (CHIPS, CHIPS, Z, Z, CHIPS, CHIPS, Z, Z):
        scratch += [dma((count,)), dma((count,))]
    out = pl.pallas_call(
        kernel,
        out_shape=jax.ShapeDtypeStruct((OUT, CENT), f32),
        in_specs=[any_space] * 5,
        out_specs=pl.BlockSpec(memory_space=pltpu.VMEM),
        scratch_shapes=scratch,
        compiler_params=pltpu.CompilerParams(
            collective_id=0, has_side_effects=True, vmem_limit_bytes=60 * 1024 * 1024
        ),
        name="falkon",
    )(features, centers, labels, coeffs, precond)
    return out.T


def solution(mesh):
    in_specs = (
        P("rows", None),
        P("centers", None),
        P("rows", None),
        P("centers", None),
        P("rows", "centers"),
    )
    return jax.shard_map(body, mesh=mesh, in_specs=in_specs, out_specs=P("centers", None), check_vma=False)
```

profile of v0, /device:TPU:1, one launch (start us, length us, event | category | flops | bytes accessed | tf_op | source)
XLA Modules:
  0.0 120.8 jit_solution(1705509042039056825)
XLA Ops:
  0.0 1.7 %copy.7.coef_hbm = f32[512,64]{1,0:T(8,128)} copy(f32[512,64]{0,1:T(8,128)} %param.8) | data formatting | bytes 262144 | tf_op args[3]
  1.7 1.9 %copy.6.lab_hbm = s32[1024,64]{1,0:T(8,128)} copy(s32[1024,64]{0,1:T(8,128)} %param.7) | data formatting | bytes 524288 | tf_op args[2]
  3.7 115.6 %falkon.1 = f32[64,512]{1,0:T(8,128)} custom-call(f32[1024,128]{1,0:T(8,128)} %feat_hbm.1, f32[512,128]{1,0:T(8,128)} %cent_hbm.1, s32[1024,64]{1,0:T(8,128)} %copy.6.lab_hbm, f32[512,64]{1,0:T(8,128)} %copy.7.coef_hbm, f32[2048,512]{1,0:T(8,128)} %prec_hbm.1), custom_call_target="tpu_custom_call" | custom-call | tf_op jit(solution)/shard_map/falkon/pallas_call | solution.py:376
  119.3 1.6 %copy.9 = f32[512,64]{0,1:T(8,128)} copy(f32[512,64]{0,1:T(8,128)} %bitcast.1) | data formatting | bytes 262144
where the time goes:
time: 121 us
  Pallas kernels  116 us (96%)
  local copies, waits for them, and re-layouts  5.25 us (4%)
    pallas_call x1, Pallas kernels, body(): pl.pallas_call(kernel, out_shape=jax.ShapeDtypeStruct((OUT, CENT), f32),...  116 us
    unnamed x3, local copies, waits for them, and re-layouts  5.25 us

commit v1 on v0

v1 whole, which is shorter than its diff:
```python
import functools

import jax
import jax.numpy as jnp
from jax import lax
from jax.experimental import pallas as pl
from jax.experimental.pallas import tpu as pltpu
from jax.sharding import PartitionSpec as P

STEPS = 2
step_size = 0.5
epsilon = 1e-06
LOG2E = 1.4426950408889634

Z, Y, X = 8, 4, 4
CHIPS = Y * X
D = 128
OUT = 64
OUTS = OUT // 2
GROUPS = OUTS // 8
ROWS = 1024
CENT = 512
PROWS = 2048
RS_ROWS = ROWS // X
RS_PROWS = PROWS // X
FAR_FIRST = (2, 1, 3, 0)
NEAR_FIRST = (0, 1, 3, 2)
Z_EVEN = (4, 2, 6)
Z_ODD = (3, 5, 1, 7)
f32 = jnp.float32
bf16 = jnp.bfloat16
MESH = pl.DeviceIdType.MESH


def split(x):
    hi = x.astype(bf16)
    lo = (x - hi.astype(f32)).astype(bf16)
    return hi, lo


def split3(x):
    hi = x.astype(bf16)
    rest = x - hi.astype(f32)
    mid = rest.astype(bf16)
    lo = (rest - mid.astype(f32)).astype(bf16)
    return hi, mid, lo


def stacked(x):
    hi, lo = split(x)
    return jnp.concatenate([hi, lo], axis=0), hi


def dot(a, b, contract):
    return lax.dot_general(a, b, (((1,), (contract,)), ((), ())), preferred_element_type=f32)


def product(lhs, w_hi, w_lo, contract):
    both, hi = lhs
    n = hi.shape[0]
    r = dot(both, w_hi, contract)
    s = dot(hi, w_lo, contract)
    return r[:n] + r[n:] + s


def kernel(
    feat_hbm, cent_hbm, lab_hbm, coef_hbm, prec_hbm, out_ref,
    feat, cent, lab, coef, coef_pair, r1, r2, r3, l1, l2, norm, k_hi, k_lo, p_raw, p_hi, p_lo,
    pair_s, pair_r, log_a, gra_a, fwd_a, bak_a,
    log_p, log_r, res_f, gra_p, gra_r, gra_f, fwd_p, fwd_r, fwd_f, bak_p, bak_r, a_f, sq_s, sq_r, fin,
    load_sem, pair_send, pair_recv, pch_send, pch_recv,
    log_ss, log_rs, res_ss, res_rs, gra_ss, gra_rs, grf_ss, grf_rs,
    fwd_ss, fwd_rs, fwf_ss, fwf_rs, bak_ss, bak_rs, af_ss, af_rs, sq_ss, sq_rs, fin_ss, fin_rs,
):
    z = lax.axis_index("rows")
    c = lax.axis_index("centers")
    j = c // 2
    k = c % 2
    y = j // X
    x = j % X
    zlo = z % 2
    other = 1 - k
    partner = c + 1 - 2 * k
    mine = pl.multiple_of(k * OUTS, OUTS)
    theirs = pl.multiple_of(other * OUTS, OUTS)

    lab_at = (
        pl.ds(pl.multiple_of(k * OUTS + y * 8, 8), 8),
        pl.ds(pl.multiple_of(x * RS_ROWS, RS_ROWS), RS_ROWS),
    )
    loads = [
        pltpu.make_async_copy(feat_hbm, feat, load_sem.at[0]),
        pltpu.make_async_copy(cent_hbm, cent.at[k], load_sem.at[1]),
        pltpu.make_async_copy(coef_hbm, coef, load_sem.at[2]),
        pltpu.make_async_copy(lab_hbm.at[lab_at], lab, load_sem.at[3]),
        pltpu.make_async_copy(prec_hbm, p_raw.at[k], load_sem.at[4]),
    ]
    for copy in loads:
        copy.start()

    barrier = pltpu.get_barrier_semaphore()
    pl.semaphore_signal(barrier, inc=1, device_id=(z, partner), device_id_type=MESH)

    def chip_at(dy, dx):
        return lax.rem(y + dy, Y) * X + lax.rem(x + dx, X)

    plane = [(dy, dx) for dx in FAR_FIRST for dy in FAR_FIRST if (dy, dx) != (0, 0)]
    for dy, dx in plane:
        pl.semaphore_signal(barrier, inc=1, device_id=(z, 2 * chip_at(dy, dx) + k), device_id_type=MESH)
    for oz in Z_EVEN + Z_ODD:
        pl.semaphore_signal(barrier, inc=1, device_id=(lax.rem(z + oz, Z), c), device_id_type=MESH)
        pl.semaphore_signal(barrier, inc=1, device_id=(lax.rem(z + oz, Z), partner), device_id_type=MESH)

    def remote(src, dst, send, recv, device):
        return pltpu.make_async_remote_copy(
            src_ref=src, dst_ref=dst, send_sem=send, recv_sem=recv, device_id=device, device_id_type=MESH
        )

    def to_pair(src, dst, n):
        return remote(src, dst, pair_send.at[n], pair_recv.at[n], (z, partner))

    def to_plane(src, dst, ss, rs, dy, dx):
        o = dy * X + dx
        return remote(src, dst, ss.at[o], rs.at[o], (z, 2 * chip_at(dy, dx) + k))

    def to_z(src, dst, ss, rs, oz):
        return remote(src, dst, ss.at[oz], rs.at[oz], (lax.rem(z + oz, Z), c))

    factor = 2.0 * LOG2E / D
    loads[0].wait()
    fx = feat[...]
    hi, mid, lo = split3(fx)
    r1[...] = jnp.concatenate([hi, hi], axis=1)
    r2[...] = jnp.concatenate([mid, mid], axis=1)
    r3[...] = jnp.concatenate([lo, hi], axis=1)
    hi, mid, lo = split3(fx * fx)
    ones = jnp.ones((16, D), bf16)
    row_norm = dot(ones, hi, 1) + dot(ones, mid, 1) + dot(ones, lo, 1)
    norm[...] = row_norm[:8] * factor

    def kernel_half(h):
        cx = cent[h]
        hi, mid, lo = split3(cx)
        l1[...] = jnp.concatenate([hi, mid], axis=1)
        l2[...] = jnp.concatenate([hi, lo], axis=1)
        cn = jnp.sum(cx * cx, axis=1, keepdims=True) * factor

        @pl.loop(0, X)
        def _(i):
            at = pl.ds(pl.multiple_of(i * RS_ROWS, RS_ROWS), RS_ROWS)
            cross = dot(l1[...], r1[at, :], 1) + dot(l1[...], r2[at, :], 1) + dot(l2[...], r3[at, :], 1)
            tile = jnp.exp2(cross * (2.0 * factor) - (cn + norm[:1, at]))
            hi, lo = split(tile)
            k_hi[h, :, at] = hi
            k_lo[h, :, at] = lo

    def precond_half(h):
        @pl.loop(0, PROWS // 128)
        def _(i):
            at = pl.multiple_of(i * 128, 128)
            hi, lo = split(p_raw[h, pl.ds(at, 128), :])
            p_hi[h, pl.ds(at, 128), :] = hi
            p_lo[h, pl.ds(at, 128), :] = lo

    precond_chunks = [
        remote(
            p_raw.at[k, pl.ds(i * 256, 256), :], p_raw.at[k, pl.ds(i * 256, 256), :],
            pch_send.at[i], pch_recv.at[i], (z, partner),
        )
        for i in range(8)
    ]

    loads[1].wait()
    kernel_half(k)
    loads[2].wait()

    def half_of(pieces, h):
        return jnp.concatenate([pieces[og * 2 + h] for og in range(GROUPS)], axis=0)

    def line_of(pieces, rg):
        return jnp.concatenate([pieces[og * X + rg] for og in range(GROUPS)], axis=0)

    for step in range(STEPS):
        sends = []

        def send_logits(dx, part):
            rg = lax.rem(x + dx, X)
            for og in range(GROUPS):
                log_p[og * X + rg] = part[og * 8 : og * 8 + 8]
            for dy in FAR_FIRST:
                if (dy, dx) != (0, 0):
                    copy = to_plane(log_p.at[chip_at(dy, dx)], log_r.at[dy * X + dx], log_ss, log_rs, dy, dx)
                    copy.start()
                    sends.append(copy)

        def rows_at(dx):
            return pl.ds(pl.multiple_of(lax.rem(x + dx, X) * RS_ROWS, RS_ROWS), RS_ROWS)

        if step == 0:
            lhs = stacked(jnp.concatenate([coef[pl.ds(theirs, OUTS), :], coef[pl.ds(mine, OUTS), :]], axis=0))
            for n, dx in enumerate(FAR_FIRST):
                part = product(lhs, k_hi[k, :, rows_at(dx)], k_lo[k, :, rows_at(dx)], 0)
                pair_s[n] = part[:OUTS]
                log_a[n] = part[OUTS:]
            pl.semaphore_wait(barrier, 1 + len(plane) + 2 * (Z - 1))
            pairs = [to_pair(pair_s.at[n], pair_r.at[n], n) for n in range(X)]
            for copy in pairs:
                copy.start()
            cent_pair = to_pair(cent.at[k], cent.at[k], 4)
            cent_pair.start()
            coef_copy = to_pair(coef.at[pl.ds(theirs, OUTS), :], coef_pair, 5)
            coef_copy.start()
            for n, dx in enumerate(FAR_FIRST):
                pairs[n].wait_recv()
                send_logits(dx, log_a[n] + pair_r[n])
            loads[4].wait()
            for copy in precond_chunks[:4]:
                copy.start()
            for copy in pairs:
                copy.wait_send()
            cent_pair.wait()
            kernel_half(other)
            coef_copy.wait()
            for og in range(GROUPS):
                a_f[og * 2 + k] = coef[pl.ds(mine + og * 8, 8), :]
                a_f[og * 2 + other] = coef_pair[og * 8 : og * 8 + 8, :]
            precond_half(k)
            loads[3].wait()
        else:
            for rel, offsets in ((1, Z_ODD), (0, Z_EVEN)):
                for copy in gathers[rel]:
                    copy.wait_recv()
                h = lax.rem(zlo + rel, 2)
                lhs = stacked(half_of(a_f, h))
                for n, dx in enumerate(FAR_FIRST):
                    part = product(lhs, k_hi[h, :, rows_at(dx)], k_lo[h, :, rows_at(dx)], 0)
                    if rel:
                        log_a[n] = part
                    else:
                        send_logits(dx, log_a[n] + part)
            for rel in range(2):
                for copy in gathers[rel]:
                    copy.wait_send()
        total = log_p[j]
        for copy, (dy, dx) in reversed(list(zip(sends, plane))):
            copy.wait_recv()
            total = total + log_r[dy * X + dx]
        res_f[j] = (jax.nn.sigmoid(total) - lab[...].astype(f32)) * (1.0 / (ROWS * Z))

        gathers = {}
        for dy, dx in plane:
            copy = to_plane(res_f.at[j], res_f.at[j], res_ss, res_rs, dy, dx)
            copy.start()
            gathers.setdefault(dx, []).append(copy)
        if step == 0:
            for copy in precond_chunks[4:]:
                copy.start()
        for copy in sends:
            copy.wait_send()

        sends = []
        for dx in NEAR_FIRST:
            for copy in reversed(gathers[dx]):
                copy.wait_recv()
            rg = lax.rem(x - dx + X, X)
            lhs = stacked(line_of(res_f, rg))
            rows = pl.ds(pl.multiple_of(rg * RS_ROWS, RS_ROWS), RS_ROWS)
            for rel, offsets in ((0, Z_EVEN), (1, Z_ODD)):
                cg = lax.rem(zlo + rel, 2)
                for s in range(2):
                    at = slice(s * 256, s * 256 + 256)
                    part = product(lhs, k_hi[cg, at, rows], k_lo[cg, at, rows], 1)
                    if dx != NEAR_FIRST[0]:
                        part = gra_a[rel, :, at] + part
                    if dx != NEAR_FIRST[-1]:
                        gra_a[rel, :, at] = part
                    else:
                        for og in range(GROUPS):
                            gra_p[og * 2 + cg, :, at] = part[og * 8 : og * 8 + 8]
                if dx == NEAR_FIRST[-1]:
                    for oz in offsets:
                        copy = to_z(gra_p.at[lax.rem(z + oz, Z)], gra_r.at[oz], gra_ss, gra_rs, oz)
                        copy.start()
                        sends.append((oz, copy))
        for dx in NEAR_FIRST:
            for copy in gathers[dx]:
                copy.wait_send()
        if step == 0:
            for copy in precond_chunks:
                copy.wait()
            precond_half(other)
        total = gra_p[z]
        for oz, copy in reversed(sends):
            copy.wait_recv()
            total = total + gra_r[oz]
        gra_f[z] = total
        gathers = {0: [], 1: []}
        for oz in Z_EVEN + Z_ODD:
            copy = to_z(gra_f.at[z], gra_f.at[z], grf_ss, grf_rs, oz)
            copy.start()
            gathers[oz % 2].append(copy)
        for oz, copy in sends:
            copy.wait_send()

        sends = []
        for rel in (1, 0):
            for copy in gathers[rel]:
                copy.wait_recv()
            h = lax.rem(zlo + rel, 2)
            lhs = stacked(half_of(gra_f, h))
            for n, dx in enumerate(FAR_FIRST):
                rg = lax.rem(x + dx, X)
                for s in range(2):
                    at = pl.ds(pl.multiple_of(rg * RS_PROWS + s * 256, 256), 256)
                    col = slice(s * 256, s * 256 + 256)
                    part = product(lhs, p_hi[h, at, :], p_lo[h, at, :], 1)
                    if rel:
                        fwd_a[n, :, col] = part
                    else:
                        part = fwd_a[n, :, col] + part
                        for og in range(GROUPS):
                            fwd_p[og * X + rg, :, col] = part[og * 8 : og * 8 + 8]
                if not rel:
                    for dy in FAR_FIRST:
                        if (dy, dx) != (0, 0):
                            copy = to_plane(
                                fwd_p.at[chip_at(dy, dx)], fwd_r.at[dy * X + dx], fwd_ss, fwd_rs, dy, dx
                            )
                            copy.start()
                            sends.append(copy)
        for rel in range(2):
            for copy in gathers[rel]:
                copy.wait_send()
        total = fwd_p[j]
        for copy, (dy, dx) in reversed(list(zip(sends, plane))):
            copy.wait_recv()
            total = total + fwd_r[dy * X + dx]
        fwd_f[j] = total
        gathers = {}
        for dy, dx in plane:
            copy = to_plane(fwd_f.at[j], fwd_f.at[j], fwf_ss, fwf_rs, dy, dx)
            copy.start()
            gathers.setdefault(dx, []).append(copy)
        for copy in sends:
            copy.wait_send()

        sends = []
        square = jnp.zeros((8, 128), f32)
        for dx in NEAR_FIRST:
            for copy in reversed(gathers[dx]):
                copy.wait_recv()
            rg = lax.rem(x - dx + X, X)
            line = line_of(fwd_f, rg)
            for og in range(GROUPS):
                for t in range(RS_PROWS // 128):
                    tile = line[og * 8 : og * 8 + 8, t * 128 : t * 128 + 128]
                    square = square + tile * tile
            if dx == NEAR_FIRST[-1]:
                sq_s[step] = square
                for i in range(Z):
                    bak_p[i, :, CENT:] = square
                squares = [
                    remote(
                        sq_s.at[step], sq_r.at[step, oz], sq_ss.at[step, oz], sq_rs.at[step, oz],
                        (lax.rem(z + oz, Z), partner),
                    )
                    for oz in Z_EVEN + Z_ODD + (0,)
                ]
                for copy in squares:
                    copy.start()
            lhs = stacked(line)
            rows = pl.ds(pl.multiple_of(rg * RS_PROWS, RS_PROWS), RS_PROWS)
            for rel, offsets in ((0, Z_EVEN), (1, Z_ODD)):
                cg = lax.rem(zlo + rel, 2)
                for s in range(2):
                    at = slice(s * 256, s * 256 + 256)
                    part = product(lhs, p_hi[cg, rows, at], p_lo[cg, rows, at], 0)
                    if dx != NEAR_FIRST[0]:
                        part = bak_a[rel, :, at] + part
                    if dx != NEAR_FIRST[-1]:
                        bak_a[rel, :, at] = part
                    else:
                        for og in range(GROUPS):
                            bak_p[og * 2 + cg, :, at] = part[og * 8 : og * 8 + 8]
                if dx == NEAR_FIRST[-1]:
                    for oz in offsets:
                        copy = to_z(bak_p.at[lax.rem(z + oz, Z)], bak_r.at[oz], bak_ss, bak_rs, oz)
                        copy.start()
                        sends.append((oz, copy))
        for dx in NEAR_FIRST:
            for copy in gathers[dx]:
                copy.wait_send()
        total = bak_p[z]
        for oz, copy in reversed(sends):
            copy.wait_recv()
            total = total + bak_r[oz]
        square = total[:, CENT:]
        for copy in squares:
            copy.wait_recv()
        for oz in range(Z):
            square = square + sq_r[step, oz]
        square = jnp.sum(jnp.sum(square, axis=1, keepdims=True), axis=0, keepdims=True)
        scale = step_size / jnp.sqrt(square / (CENT * 2 * CHIPS * OUT) + epsilon)
        a_f[z] = a_f[z] - scale * total[:, :CENT]
        for copy in squares:
            copy.wait_send()
        if step < STEPS - 1:
            gathers = {0: [], 1: []}
            for oz in Z_EVEN + Z_ODD:
                copy = to_z(a_f.at[z], a_f.at[z], af_ss, af_rs, oz)
                copy.start()
                gathers[oz % 2].append(copy)
        for oz, copy in sends:
            copy.wait_send()

    og = z // 2
    rel = lax.rem(k + zlo, 2)
    piece = k * GROUPS + og

    def to_holder(oz, r):
        return remote(
            a_f.at[z], fin.at[piece], fin_ss.at[oz], fin_rs.at[oz * 2 + r], (lax.rem(z + oz, Z), 2 * j + zlo)
        )

    def from_holder(oz, r):
        source = (k + r * (1 - 2 * k)) * GROUPS + lax.rem(z - oz + Z, Z) // 2
        remote(a_f.at[z], fin.at[source], fin_ss.at[oz], fin_rs.at[oz * 2 + r], (z, partner)).wait_recv()

    copies = [to_holder(oz, rel) for oz in Z_EVEN + Z_ODD]
    for copy in copies:
        copy.start()

    @pl.when(rel == 0)
    def _():
        fin[piece] = a_f[z]
        from_holder(0, 1)
        for oz in Z_EVEN:
            for r in range(2):
                from_holder(oz, r)

    @pl.when(rel == 1)
    def _():
        to_holder(0, 1).start()
        for oz in Z_ODD:
            for r in range(2):
                from_holder(oz, r)
        to_holder(0, 1).wait_send()

    for copy in copies:
        copy.wait_send()
    for i in range(OUT // 8):
        out_ref[i * 8 : i * 8 + 8, :] = fin[i]


def body(features, centers, labels, coeffs, precond):
    any_space = pl.BlockSpec(memory_space=pl.ANY)
    V = pltpu.VMEM
    dma = pltpu.SemaphoreType.DMA
    scratch = [
        V((ROWS, D), f32),
        V((2, CENT, D), f32),
        V((8, RS_ROWS), jnp.int32),
        V((OUT, CENT), f32),
        V((OUTS, CENT), f32),
        V((ROWS, 2 * D), bf16),
        V((ROWS, 2 * D), bf16),
        V((ROWS, 2 * D), bf16),
        V((CENT, 2 * D), bf16),
        V((CENT, 2 * D), bf16),
        V((8, ROWS), f32),
        V((2, CENT, ROWS), bf16),
        V((2, CENT, ROWS), bf16),
        V((2, PROWS, CENT), f32),
        V((2, PROWS, CENT), bf16),
        V((2, PROWS, CENT), bf16),
        V((X, OUTS, RS_ROWS), f32),
        V((X, OUTS, RS_ROWS), f32),
        V((X, OUTS, RS_ROWS), f32),
        V((2, OUTS, CENT), f32),
        V((X, OUTS, RS_PROWS), f32),
        V((2, OUTS, CENT), f32),
        V((CHIPS, 8, RS_ROWS), f32),
        V((CHIPS, 8, RS_ROWS), f32),
        V((CHIPS, 8, RS_ROWS), f32),
        V((Z, 8, CENT), f32),
        V((Z, 8, CENT), f32),
        V((Z, 8, CENT), f32),
        V((CHIPS, 8, RS_PROWS), f32),
        V((CHIPS, 8, RS_PROWS), f32),
        V((CHIPS, 8, RS_PROWS), f32),
        V((Z, 8, CENT + 128), f32),
        V((Z, 8, CENT + 128), f32),
        V((Z, 8, CENT), f32),
        V((STEPS, 8, 128), f32),
        V((STEPS, Z, 8, 128), f32),
        V((OUT // 8, 8, CENT), f32),
        dma((5,)),
        dma((9,)),
        dma((9,)),
        dma((8,)),
        dma((8,)),
    ]
    for count in (CHIPS, CHIPS, Z, Z, CHIPS, CHIPS, Z, Z):
        scratch += [dma((count,)), dma((count,))]
    scratch += [dma((STEPS, Z)), dma((STEPS, Z)), dma((Z,)), dma((2 * Z,))]
    out = pl.pallas_call(
        kernel,
        out_shape=pltpu.VMEM((OUT, CENT), f32),
        in_specs=[any_space] * 5,
        out_specs=pl.BlockSpec(memory_space=pltpu.VMEM),
        scratch_shapes=scratch,
        compiler_params=pltpu.CompilerParams(
            collective_id=0, has_side_effects=True, vmem_limit_bytes=60 * 1024 * 1024
        ),
        name="falkon",
    )(features, centers, labels.T, coeffs.T, precond)
    return out.T


def solution(mesh):
    in_specs = (
        P("rows", None),
        P("centers", None),
        P("rows", None),
        P("centers", None),
        P("rows", "centers"),
    )
    return jax.shard_map(body, mesh=mesh, in_specs=in_specs, out_specs=P("centers", None), check_vma=False)
```

time: 121 us -> 108 us (0.89)
  Pallas kernels: 116 us -> 107 us
  local copies, waits for them, and re-layouts: 5.25 us -> 0.66 us
    pallas_call x1, Pallas kernels: 116 us -> 107 us  [body(): pl.pallas_call(kernel, out_shape=pltpu.VMEM((OUT, CENT), f32), in_specs=[...]
    unnamed x3 -> x1, local copies, waits for them, and re-layouts: 5.25 us -> 0.66 us
where the time goes in v1:
time: 108 us
  Pallas kernels  107 us (99%)
    pallas_call x1, Pallas kernels, body(): pl.pallas_call(kernel, out_shape=pltpu.VMEM((OUT, CENT), f32), in_specs=[...  107 us

profile of v1, /device:TPU:1, one launch (start us, length us, event | category | flops | bytes accessed | tf_op | source)
XLA Modules:
  0.0 107.7 jit_solution(8798086551651691470)
XLA Ops:
  0.0 107.1 %falkon.1 = f32[64,512]{1,0:T(8,128)S(1)} custom-call(f32[1024,128]{1,0:T(8,128)} %feat_hbm.1, f32[512,128]{1,0:T(8,128)} %cent_hbm.1, s32[64,1024]{1,0:T(8,128)} %bitcast.4, f32[64,512]{1,0:T(8,128)} %bitcast.5, f32[2048,512]{1,0:T(8,128)} %prec_hbm.1), custom_call_target="tpu_custom_call" | custom-call | tf_op jit(solution)/shard_map/falkon/pallas_call | solution.py:506
  107.1 0.7 copy.7

commit v2 on v1

v2 whole, which is shorter than its diff:
```python
import functools

import jax
import jax.numpy as jnp
from jax import lax
from jax.experimental import pallas as pl
from jax.experimental.pallas import tpu as pltpu
from jax.sharding import PartitionSpec as P

STEPS = 2
step_size = 0.5
epsilon = 1e-06
LOG2E = 1.4426950408889634

Z, Y, X = 8, 4, 4
CHIPS = Y * X
D = 128
OUT = 64
OUTS = OUT // 2
GROUPS = OUTS // 8
ROWS = 1024
CENT = 512
PROWS = 2048
RS_ROWS = ROWS // X
RS_PROWS = PROWS // X
FAR_FIRST = (2, 1, 3, 0)
NEAR_FIRST = (0, 1, 3, 2)
Z_FAR = (4, 3, 5, 2, 6, 1, 7)
PLANE_FAR = (
    (2, 2), (1, 2), (2, 1), (3, 2), (2, 3), (1, 1), (3, 3), (1, 3), (3, 1), (2, 0), (0, 2), (1, 0), (0, 1), (3, 0), (0, 3),
)
PAIRS = Z // 2
PAIR = 2 * CENT // PAIRS
PIECE = PAIR // 2
f32 = jnp.float32
bf16 = jnp.bfloat16
MESH = pl.DeviceIdType.MESH


def split(x):
    hi = x.astype(bf16)
    lo = (x - hi.astype(f32)).astype(bf16)
    return hi, lo


def split3(x):
    hi = x.astype(bf16)
    rest = x - hi.astype(f32)
    mid = rest.astype(bf16)
    lo = (rest - mid.astype(f32)).astype(bf16)
    return hi, mid, lo


def stacked(x):
    hi, lo = split(x)
    return jnp.concatenate([hi, lo], axis=0), hi


def dot(a, b, contract):
    return lax.dot_general(a, b, (((1,), (contract,)), ((), ())), preferred_element_type=f32)


def product(lhs, w_hi, w_lo, contract):
    both, hi = lhs
    n = hi.shape[0]
    r = dot(both, w_hi, contract)
    s = dot(hi, w_lo, contract)
    return r[:n] + r[n:] + s


def kernel(
    feat_hbm, cent_hbm, lab_hbm, coef_hbm, prec_hbm, out_ref,
    feat, cent, lab, coef, coef_pair, r1, r2, r3, l1, l2, norm, k_hi, k_lo, p_raw, p_hi, p_lo,
    pair_s, pair_r, log_a, col_a, fwd_a,
    log_p, log_r, res_f, gra_p, gra_r, gra_f, fwd_p, fwd_r, fwd_f, bak_p, bak_r, a_f, sq_s, sq_r, fin,
    load_sem, pair_send, pair_recv, pch_send, pch_recv,
    log_ss, log_rs, res_ss, res_rs, gra_ss, gra_rs, grf_ss, grf_rs,
    fwd_ss, fwd_rs, fwf_ss, fwf_rs, bak_ss, bak_rs, af_ss, af_rs, sq_ss, sq_rs, fin_ss, fin_rs,
):
    z = lax.axis_index("rows")
    c = lax.axis_index("centers")
    j = c // 2
    k = c % 2
    y = j // X
    x = j % X
    zp = z // 2
    zlo = z % 2
    other = 1 - k
    partner = c + 1 - 2 * k
    mine = pl.multiple_of(k * OUTS, OUTS)
    theirs = pl.multiple_of(other * OUTS, OUTS)

    lab_at = (
        pl.ds(pl.multiple_of(k * OUTS + y * 8, 8), 8),
        pl.ds(pl.multiple_of(x * RS_ROWS, RS_ROWS), RS_ROWS),
    )
    loads = [
        pltpu.make_async_copy(feat_hbm, feat, load_sem.at[0]),
        pltpu.make_async_copy(cent_hbm, cent.at[k], load_sem.at[1]),
        pltpu.make_async_copy(coef_hbm, coef, load_sem.at[2]),
        pltpu.make_async_copy(lab_hbm.at[lab_at], lab, load_sem.at[3]),
        pltpu.make_async_copy(prec_hbm, p_raw.at[k], load_sem.at[4]),
    ]
    for copy in loads:
        copy.start()

    barrier = pltpu.get_barrier_semaphore()
    pl.semaphore_signal(barrier, inc=1, device_id=(z, partner), device_id_type=MESH)

    def chip_at(dy, dx):
        return lax.rem(y + dy, Y) * X + lax.rem(x + dx, X)

    plane = PLANE_FAR
    for dy, dx in plane:
        pl.semaphore_signal(barrier, inc=1, device_id=(z, 2 * chip_at(dy, dx) + k), device_id_type=MESH)
    for oz in Z_FAR:
        pl.semaphore_signal(barrier, inc=1, device_id=(lax.rem(z + oz, Z), c), device_id_type=MESH)
        pl.semaphore_signal(barrier, inc=1, device_id=(lax.rem(z + oz, Z), partner), device_id_type=MESH)

    def remote(src, dst, send, recv, device):
        return pltpu.make_async_remote_copy(
            src_ref=src, dst_ref=dst, send_sem=send, recv_sem=recv, device_id=device, device_id_type=MESH
        )

    def to_pair(src, dst, n):
        return remote(src, dst, pair_send.at[n], pair_recv.at[n], (z, partner))

    def to_plane(src, dst, ss, rs, dy, dx):
        o = dy * X + dx
        return remote(src, dst, ss.at[o], rs.at[o], (z, 2 * chip_at(dy, dx) + k))

    def to_z(src, dst, ss, rs, oz):
        return remote(src, dst, ss.at[oz], rs.at[oz], (lax.rem(z + oz, Z), c))

    factor = 2.0 * LOG2E / D
    loads[0].wait()
    fx = feat[...]
    hi, mid, lo = split3(fx)
    r1[...] = jnp.concatenate([hi, hi], axis=1)
    r2[...] = jnp.concatenate([mid, mid], axis=1)
    r3[...] = jnp.concatenate([lo, hi], axis=1)
    hi, mid, lo = split3(fx * fx)
    ones = jnp.ones((16, D), bf16)
    row_norm = dot(ones, hi, 1) + dot(ones, mid, 1) + dot(ones, lo, 1)
    norm[...] = row_norm[:8] * factor

    def kernel_half(h):
        cx = cent[h]
        hi, mid, lo = split3(cx)
        l1[...] = jnp.concatenate([hi, mid], axis=1)
        l2[...] = jnp.concatenate([hi, lo], axis=1)
        cn = jnp.sum(cx * cx, axis=1, keepdims=True) * factor

        @pl.loop(0, X)
        def _(i):
            at = pl.ds(pl.multiple_of(i * RS_ROWS, RS_ROWS), RS_ROWS)
            cross = dot(l1[...], r1[at, :], 1) + dot(l1[...], r2[at, :], 1) + dot(l2[...], r3[at, :], 1)
            tile = jnp.exp2(cross * (2.0 * factor) - (cn + norm[:1, at]))
            hi, lo = split(tile)
            k_hi[h, :, at] = hi
            k_lo[h, :, at] = lo

    def precond_half(h):
        @pl.loop(0, PROWS // 128)
        def _(i):
            at = pl.multiple_of(i * 128, 128)
            hi, lo = split(p_raw[h, pl.ds(at, 128), :])
            p_hi[h, pl.ds(at, 128), :] = hi
            p_lo[h, pl.ds(at, 128), :] = lo

    precond_chunks = [
        remote(
            p_raw.at[k, pl.ds(i * 256, 256), :], p_raw.at[k, pl.ds(i * 256, 256), :],
            pch_send.at[i], pch_recv.at[i], (z, partner),
        )
        for i in range(8)
    ]

    loads[1].wait()
    kernel_half(k)
    loads[2].wait()

    def line_of(pieces, rg):
        return jnp.concatenate([pieces[og * X + rg] for og in range(GROUPS)], axis=0)

    def pair_of(pieces, p):
        return jnp.concatenate([pieces[2 * p], pieces[2 * p + 1]], axis=1)

    def pair_at(p):
        return p // 2, pl.ds(pl.multiple_of((p % 2) * PAIR, PAIR), PAIR)

    def row_block(dx, size):
        rg = lax.rem(x + dx, X)
        return rg, pl.ds(pl.multiple_of(rg * size, size), size)

    def scatter_plane(pieces, landing, ss, rs, dx):
        for dy in FAR_FIRST:
            if (dy, dx) != (0, 0):
                to_plane(pieces.at[chip_at(dy, dx)], landing.at[dy * X + dx], ss, rs, dy, dx).start()

    def plane_sum(pieces, landing, ss, rs):
        total = pieces[j]
        for dy, dx in reversed(plane):
            to_plane(pieces.at[j], landing.at[dy * X + dx], ss, rs, dy, dx).wait_recv()
            total = total + landing[dy * X + dx]
        return total

    def gather_plane(pieces, ss, rs):
        for dy, dx in plane:
            to_plane(pieces.at[j], pieces.at[j], ss, rs, dy, dx).start()

    def arrived_line(pieces, ss, rs, dx):
        for dy in reversed(FAR_FIRST):
            if (dy, dx) != (0, 0):
                to_plane(pieces.at[j], pieces.at[chip_at(Y - dy, X - dx)], ss, rs, dy, dx).wait_recv()

    def sent_plane(pieces, ss, rs):
        for dy, dx in plane:
            to_plane(pieces.at[j], pieces.at[j], ss, rs, dy, dx).wait_send()

    def pair_members(r):
        p = lax.rem(zp + r, PAIRS)
        return p, ([2 * p, 2 * p + 1] if r else [z + 1 - 2 * zlo])

    def scatter_z(pieces, landing, ss, rs, r):
        for other_z in pair_members(r)[1]:
            oz = lax.rem(other_z - z + Z, Z)
            to_z(pieces.at[other_z], landing.at[oz], ss, rs, oz).start()

    def z_sum(pieces, landing, ss, rs):
        total = pieces[z]
        for oz in reversed(Z_FAR):
            to_z(pieces.at[z], landing.at[oz], ss, rs, oz).wait_recv()
            total = total + landing[oz]
        return total

    def gather_z(pieces, ss, rs):
        for oz in Z_FAR:
            to_z(pieces.at[z], pieces.at[z], ss, rs, oz).start()

    def arrived_pair(pieces, ss, rs, r):
        for other_z in pair_members(r)[1]:
            to_z(pieces.at[z], pieces.at[other_z], ss, rs, lax.rem(z - other_z + Z, Z)).wait_recv()

    def sent_z(pieces, ss, rs):
        for oz in Z_FAR:
            to_z(pieces.at[z], pieces.at[z], ss, rs, oz).wait_send()

    def send_logits(dx, part):
        rg = lax.rem(x + dx, X)
        for og in range(GROUPS):
            log_p[og * X + rg] = part[og * 8 : og * 8 + 8]
        scatter_plane(log_p, log_r, log_ss, log_rs, dx)

    lhs = stacked(jnp.concatenate([coef[pl.ds(theirs, OUTS), :], coef[pl.ds(mine, OUTS), :]], axis=0))
    for n, dx in enumerate(FAR_FIRST):
        rg, at = row_block(dx, RS_ROWS)
        part = product(lhs, k_hi[k, :, at], k_lo[k, :, at], 0)
        pair_s[n] = part[:OUTS]
        log_a[n] = part[OUTS:]
    pl.semaphore_wait(barrier, 1 + len(plane) + 2 * (Z - 1))
    pairs = [to_pair(pair_s.at[n], pair_r.at[n], n) for n in range(X)]
    for copy in pairs:
        copy.start()
    cent_pair = to_pair(cent.at[k], cent.at[k], 4)
    cent_pair.start()
    coef_copy = to_pair(coef.at[pl.ds(theirs, OUTS), :], coef_pair, 5)
    coef_copy.start()
    for n, dx in enumerate(FAR_FIRST):
        pairs[n].wait_recv()
        send_logits(dx, log_a[n] + pair_r[n])
    loads[4].wait()
    for copy in precond_chunks[:4]:
        copy.start()
    for copy in pairs:
        copy.wait_send()
    cent_pair.wait()
    kernel_half(other)
    coef_copy.wait()
    for i in range(CENT // PIECE):
        col = slice(i * PIECE, i * PIECE + PIECE)
        a_f[k * (Z // 2) + i] = coef[pl.ds(mine, OUTS), col]
        a_f[other * (Z // 2) + i] = coef_pair[:, col]
    precond_half(k)
    loads[3].wait()

    @pl.loop(0, STEPS)
    def _(step):
        total = plane_sum(log_p, log_r, log_ss, log_rs)
        res_f[j] = (jax.nn.sigmoid(total) - lab[...].astype(f32)) * (1.0 / (ROWS * Z))
        gather_plane(res_f, res_ss, res_rs)

        @pl.when(step == 0)
        def _():
            for copy in precond_chunks[4:]:
                copy.start()

        sent_plane(log_p, log_ss, log_rs)

        for dx in NEAR_FIRST:
            arrived_line(res_f, res_ss, res_rs, dx)
            rg, rows = row_block(X - dx, RS_ROWS)
            lhs = stacked(line_of(res_f, rg))
            for n, r in enumerate(FAR_FIRST):
                p = lax.rem(zp + r, PAIRS)
                h, at = pair_at(p)
                part = product(lhs, k_hi[h, at, rows], k_lo[h, at, rows], 1)
                if dx != NEAR_FIRST[0]:
                    part = col_a[n] + part
                if dx != NEAR_FIRST[-1]:
                    col_a[n] = part
                else:
                    gra_p[2 * p] = part[:, :PIECE]
                    gra_p[2 * p + 1] = part[:, PIECE:]
                    scatter_z(gra_p, gra_r, gra_ss, gra_rs, r)
        sent_plane(res_f, res_ss, res_rs)

        @pl.when(step == 0)
        def _():
            for copy in precond_chunks:
                copy.wait()
            precond_half(other)

        gra_f[z] = z_sum(gra_p, gra_r, gra_ss, gra_rs)
        gather_z(gra_f, grf_ss, grf_rs)
        sent_z(gra_p, gra_ss, gra_rs)

        for r in NEAR_FIRST:
            arrived_pair(gra_f, grf_ss, grf_rs, r)
            p = lax.rem(zp + r, PAIRS)
            h, at = pair_at(p)
            lhs = stacked(pair_of(gra_f, p))
            for n, dx in enumerate(FAR_FIRST):
                rg, rows = row_block(dx, RS_PROWS)
                part = product(lhs, p_hi[h, rows, at], p_lo[h, rows, at], 1)
                if r != NEAR_FIRST[0]:
                    part = fwd_a[n] + part
                if r != NEAR_FIRST[-1]:
                    fwd_a[n] = part
                else:
                    for og in range(GROUPS):
                        fwd_p[og * X + rg] = part[og * 8 : og * 8 + 8]
                    scatter_plane(fwd_p, fwd_r, fwd_ss, fwd_rs, dx)
        sent_z(gra_f, grf_ss, grf_rs)
        fwd_f[j] = plane_sum(fwd_p, fwd_r, fwd_ss, fwd_rs)
        gather_plane(fwd_f, fwf_ss, fwf_rs)
        sent_plane(fwd_p, fwd_ss, fwd_rs)

        def to_other_core(oz):
            return remote(
                sq_s.at[step], sq_r.at[step, oz], sq_ss.at[step, oz], sq_rs.at[step, oz],
                (lax.rem(z + oz, Z), partner),
            )

        square = jnp.zeros((8, 128), f32)
        for dx in NEAR_FIRST:
            arrived_line(fwd_f, fwf_ss, fwf_rs, dx)
            rg, rows = row_block(X - dx, RS_PROWS)
            line = line_of(fwd_f, rg)
            for og in range(GROUPS):
                for t in range(RS_PROWS // 128):
                    tile = line[og * 8 : og * 8 + 8, t * 128 : t * 128 + 128]
                    square = square + tile * tile
            if dx == NEAR_FIRST[-1]:
                sq_s[step] = square
                for i in range(Z):
                    bak_p[i, OUTS:] = square
                for oz in Z_FAR + (0,):
                    to_other_core(oz).start()
            lhs = stacked(line)
            for n, r in enumerate(FAR_FIRST):
                p = lax.rem(zp + r, PAIRS)
                h, at = pair_at(p)
                part = product(lhs, p_hi[h, rows, at], p_lo[h, rows, at], 0)
                if dx != NEAR_FIRST[0]:
                    part = col_a[n] + part
                if dx != NEAR_FIRST[-1]:
                    col_a[n] = part
                else:
                    bak_p[2 * p, :OUTS] = part[:, :PIECE]
                    bak_p[2 * p + 1, :OUTS] = part[:, PIECE:]
                    scatter_z(bak_p, bak_r, bak_ss, bak_rs, r)
        sent_plane(fwd_f, fwf_ss, fwf_rs)
        total = z_sum(bak_p, bak_r, bak_ss, bak_rs)
        square = total[OUTS:]
        for oz in range(Z):
            to_other_core(oz).wait_recv()
            square = square + sq_r[step, oz]
        square = jnp.sum(jnp.sum(square, axis=1, keepdims=True), axis=0, keepdims=True)
        scale = step_size / jnp.sqrt(square / (CENT * 2 * CHIPS * OUT) + epsilon)
        a_f[z] = a_f[z] - scale * total[:OUTS]

        @pl.when(step < STEPS - 1)
        def _():
            gather_z(a_f, af_ss, af_rs)

        sent_z(bak_p, bak_ss, bak_rs)
        for oz in range(Z):
            to_other_core(oz).wait_send()

        @pl.when(step < STEPS - 1)
        def _():
            for r in NEAR_FIRST:
                arrived_pair(a_f, af_ss, af_rs, r)
                p = lax.rem(zp + r, PAIRS)
                h, at = pair_at(p)
                lhs = stacked(pair_of(a_f, p))
                for n, dx in enumerate(FAR_FIRST):
                    rg, rows = row_block(dx, RS_ROWS)
                    part = product(lhs, k_hi[h, at, rows], k_lo[h, at, rows], 0)
                    if r != NEAR_FIRST[0]:
                        part = log_a[n] + part
                    if r != NEAR_FIRST[-1]:
                        log_a[n] = part
                    else:
                        send_logits(dx, part)
            sent_z(a_f, af_ss, af_rs)

    holder = z // (Z // 2)
    rel = lax.rem(k + holder, 2)

    def to_holder(oz, r):
        return remote(
            a_f.at[z], fin.at[k * (Z // 2) + lax.rem(z, Z // 2)], fin_ss.at[oz], fin_rs.at[oz * 2 + r],
            (lax.rem(z + oz, Z), 2 * j + holder),
        )

    copies = [to_holder(oz, rel) for oz in Z_FAR]
    for copy in copies:
        copy.start()

    @pl.when(rel == 0)
    def _():
        fin[k * (Z // 2) + lax.rem(z, Z // 2)] = a_f[z]

    @pl.when(rel == 1)
    def _():
        to_holder(0, 1).start()
        to_holder(0, 1).wait_send()

    for i in range(Z // 2):
        source = k * (Z // 2) + i
        oz = lax.rem(z - source + Z, Z)

        def arrived(r):
            owner = k + r * (1 - 2 * k)
            remote(
                a_f.at[z], fin.at[owner * (Z // 2) + i], fin_ss.at[oz], fin_rs.at[oz * 2 + r], (z, partner)
            ).wait_recv()

        pl.when(source != z)(functools.partial(arrived, 0))
        arrived(1)
    for copy in copies:
        copy.wait_send()
    for n in range(2):
        for i in range(Z // 2):
            out_ref[n * OUTS : n * OUTS + OUTS, i * PIECE : i * PIECE + PIECE] = fin[n * (Z // 2) + i]


def body(features, centers, labels, coeffs, precond):
    any_space = pl.BlockSpec(memory_space=pl.ANY)
    V = pltpu.VMEM
    dma = pltpu.SemaphoreType.DMA
    scratch = [
        V((ROWS, D), f32),
        V((2, CENT, D), f32),
        V((8, RS_ROWS), jnp.int32),
        V((OUT, CENT), f32),
        V((OUTS, CENT), f32),
        V((ROWS, 2 * D), bf16),
        V((ROWS, 2 * D), bf16),
        V((ROWS, 2 * D), bf16),
        V((CENT, 2 * D), bf16),
        V((CENT, 2 * D), bf16),
        V((8, ROWS), f32),
        V((2, CENT, ROWS), bf16),
        V((2, CENT, ROWS), bf16),
        V((2, PROWS, CENT), f32),
        V((2, PROWS, CENT), bf16),
        V((2, PROWS, CENT), bf16),
        V((X, OUTS, RS_ROWS), f32),
        V((X, OUTS, RS_ROWS), f32),
        V((X, OUTS, RS_ROWS), f32),
        V((PAIRS, OUTS, PAIR), f32),
        V((X, OUTS, RS_PROWS), f32),
        V((CHIPS, 8, RS_ROWS), f32),
        V((CHIPS, 8, RS_ROWS), f32),
        V((CHIPS, 8, RS_ROWS), f32),
        V((Z, OUTS, PIECE), f32),
        V((Z, OUTS, PIECE), f32),
        V((Z, OUTS, PIECE), f32),
        V((CHIPS, 8, RS_PROWS), f32),
        V((CHIPS, 8, RS_PROWS), f32),
        V((CHIPS, 8, RS_PROWS), f32),
        V((Z, OUTS + 8, PIECE), f32),
        V((Z, OUTS + 8, PIECE), f32),
        V((Z, OUTS, PIECE), f32),
        V((STEPS, 8, 128), f32),
        V((STEPS, Z, 8, 128), f32),
        V((Z, OUTS, PIECE), f32),
        dma((5,)),
        dma((9,)),
        dma((9,)),
        dma((8,)),
        dma((8,)),
    ]
    for count in (CHIPS, CHIPS, Z, Z, CHIPS, CHIPS, Z, Z):
        scratch += [dma((count,)), dma((count,))]
    scratch += [dma((STEPS, Z)), dma((STEPS, Z)), dma((Z,)), dma((2 * Z,))]
    out = pl.pallas_call(
        kernel,
        out_shape=pltpu.VMEM((OUT, CENT), f32),
        in_specs=[any_space] * 5,
        out_specs=pl.BlockSpec(memory_space=pltpu.VMEM),
        scratch_shapes=scratch,
        compiler_params=pltpu.CompilerParams(
            collective_id=0, has_side_effects=True, vmem_limit_bytes=60 * 1024 * 1024
        ),
        name="falkon",
    )(features, centers, labels.T, coeffs.T, precond)
    return out.T


def solution(mesh):
    in_specs = (
        P("rows", None),
        P("centers", None),
        P("rows", None),
        P("centers", None),
        P("rows", "centers"),
    )
    return jax.shard_map(body, mesh=mesh, in_specs=in_specs, out_specs=P("centers", None), check_vma=False)
```

time: 108 us -> 105 us (0.972)
  Pallas kernels: 107 us -> 104 us
    pallas_call x1, Pallas kernels: 107 us -> 104 us  [body(): pl.pallas_call(kernel, out_shape=pltpu.VMEM((OUT, CENT), f32), in_specs=[...]
where the time goes in v2:
time: 105 us
  Pallas kernels  104 us (99%)
    pallas_call x1, Pallas kernels, body(): pl.pallas_call(kernel, out_shape=pltpu.VMEM((OUT, CENT), f32), in_specs=[...  104 us

profile of v2, /device:TPU:1, one launch (start us, length us, event | category | flops | bytes accessed | tf_op | source)
XLA Modules:
  0.0 105.0 jit_solution(6353899781447381352)
XLA Ops:
  0.0 104.4 %falkon.1 = f32[64,512]{1,0:T(8,128)S(1)} custom-call(f32[1024,128]{1,0:T(8,128)} %feat_hbm.1, f32[512,128]{1,0:T(8,128)} %cent_hbm.1, s32[64,1024]{1,0:T(8,128)} %bitcast.4, f32[64,512]{1,0:T(8,128)} %bitcast.5, f32[2048,512]{1,0:T(8,128)} %prec_hbm.1), custom_call_target="tpu_custom_call" | custom-call | tf_op jit(solution)/shard_map/falkon/pallas_call | solution.py:510
  104.4 0.7 copy.7

commit v3 on v2

--- a/solution.py
+++ b/solution.py
@@ -29,6 +29,7 @@
 PLANE_FAR = (
     (2, 2), (1, 2), (2, 1), (3, 2), (2, 3), (1, 1), (3, 3), (1, 3), (3, 1), (2, 0), (0, 2), (1, 0), (0, 1), (3, 0), (0, 3),
 )
+RING = tuple((oz, r) for oz in Z_FAR for r in range(2)) + ((0, 1),)
 PAIRS = Z // 2
 PAIR = 2 * CENT // PAIRS
 PIECE = PAIR // 2
@@ -70,7 +71,7 @@
 
 def kernel(
     feat_hbm, cent_hbm, lab_hbm, coef_hbm, prec_hbm, out_ref,
-    feat, cent, lab, coef, coef_pair, r1, r2, r3, l1, l2, norm, k_hi, k_lo, p_raw, p_hi, p_lo,
+    feat, cent, lab, coef, coef_pair, r1, r2, r3, l1, l2, norm, k_hi, k_lo, kt_hi, kt_lo, p_raw, p_hi, p_lo, pt_hi, pt_lo,
     pair_s, pair_r, log_a, col_a, fwd_a,
     log_p, log_r, res_f, gra_p, gra_r, gra_f, fwd_p, fwd_r, fwd_f, bak_p, bak_r, a_f, sq_s, sq_r, fin,
     load_sem, pair_send, pair_recv, pch_send, pch_recv,
@@ -90,6 +91,23 @@
     mine = pl.multiple_of(k * OUTS, OUTS)
     theirs = pl.multiple_of(other * OUTS, OUTS)
 
+    def chip_at(dy, dx):
+        return lax.rem(y + dy, Y) * X + lax.rem(x + dx, X)
+
+    barrier = pltpu.get_barrier_semaphore()
+
+    def greet(device):
+        pl.semaphore_signal(barrier, inc=1, device_id=device, device_id_type=MESH)
+
+    plane = PLANE_FAR
+    for n, (dy, dx) in enumerate(plane):
+        greet((z, 2 * chip_at(dy, dx) + k))
+        if n < len(Z_FAR):
+            oz = lax.rem(z + Z_FAR[n], Z)
+            greet((oz, c))
+            greet((oz, partner))
+    greet((z, partner))
+
     lab_at = (
         pl.ds(pl.multiple_of(k * OUTS + y * 8, 8), 8),
         pl.ds(pl.multiple_of(x * RS_ROWS, RS_ROWS), RS_ROWS),
@@ -104,19 +122,6 @@
     for copy in loads:
         copy.start()
 
-    barrier = pltpu.get_barrier_semaphore()
-    pl.semaphore_signal(barrier, inc=1, device_id=(z, partner), device_id_type=MESH)
-
-    def chip_at(dy, dx):
-        return lax.rem(y + dy, Y) * X + lax.rem(x + dx, X)
-
-    plane = PLANE_FAR
-    for dy, dx in plane:
-        pl.semaphore_signal(barrier, inc=1, device_id=(z, 2 * chip_at(dy, dx) + k), device_id_type=MESH)
-    for oz in Z_FAR:
-        pl.semaphore_signal(barrier, inc=1, device_id=(lax.rem(z + oz, Z), c), device_id_type=MESH)
-        pl.semaphore_signal(barrier, inc=1, device_id=(lax.rem(z + oz, Z), partner), device_id_type=MESH)
-
     def remote(src, dst, send, recv, device):
         return pltpu.make_async_remote_copy(
             src_ref=src, dst_ref=dst, send_sem=send, recv_sem=recv, device_id=device, device_id_type=MESH
@@ -159,14 +164,21 @@
             hi, lo = split(tile)
             k_hi[h, :, at] = hi
             k_lo[h, :, at] = lo
+            hi, lo = split(tile.T)
+            kt_hi[h, at, :] = hi
+            kt_lo[h, at, :] = lo
 
     def precond_half(h):
         @pl.loop(0, PROWS // 128)
         def _(i):
             at = pl.multiple_of(i * 128, 128)
-            hi, lo = split(p_raw[h, pl.ds(at, 128), :])
+            tile = p_raw[h, pl.ds(at, 128), :]
+            hi, lo = split(tile)
             p_hi[h, pl.ds(at, 128), :] = hi
             p_lo[h, pl.ds(at, 128), :] = lo
+            hi, lo = split(tile.T)
+            pt_hi[h, :, pl.ds(at, 128)] = hi
+            pt_lo[h, :, pl.ds(at, 128)] = lo
 
     precond_chunks = [
         remote(
@@ -304,7 +316,7 @@
             for n, r in enumerate(FAR_FIRST):
                 p = lax.rem(zp + r, PAIRS)
                 h, at = pair_at(p)
-                part = product(lhs, k_hi[h, at, rows], k_lo[h, at, rows], 1)
+                part = product(lhs, kt_hi[h, rows, at], kt_lo[h, rows, at], 0)
                 if dx != NEAR_FIRST[0]:
                     part = col_a[n] + part
                 if dx != NEAR_FIRST[-1]:
@@ -332,7 +344,7 @@
             lhs = stacked(pair_of(gra_f, p))
             for n, dx in enumerate(FAR_FIRST):
                 rg, rows = row_block(dx, RS_PROWS)
-                part = product(lhs, p_hi[h, rows, at], p_lo[h, rows, at], 1)
+                part = product(lhs, pt_hi[h, at, rows], pt_lo[h, at, rows], 0)
                 if r != NEAR_FIRST[0]:
                     part = fwd_a[n] + part
                 if r != NEAR_FIRST[-1]:
@@ -346,10 +358,11 @@
         gather_plane(fwd_f, fwf_ss, fwf_rs)
         sent_plane(fwd_p, fwd_ss, fwd_rs)
 
-        def to_other_core(oz):
+        def square_to(oz, r):
+            n = oz * 2 + r
             return remote(
-                sq_s.at[step], sq_r.at[step, oz], sq_ss.at[step, oz], sq_rs.at[step, oz],
-                (lax.rem(z + oz, Z), partner),
+                sq_s.at[step], sq_r.at[step, n], sq_ss.at[step, n], sq_rs.at[step, n],
+                (lax.rem(z + oz, Z), partner if r else c),
             )
 
         square = jnp.zeros((8, 128), f32)
@@ -362,11 +375,10 @@
                     tile = line[og * 8 : og * 8 + 8, t * 128 : t * 128 + 128]
                     square = square + tile * tile
             if dx == NEAR_FIRST[-1]:
+                square = jnp.sum(square, axis=0, keepdims=True)
                 sq_s[step] = square
-                for i in range(Z):
-                    bak_p[i, OUTS:] = square
-                for oz in Z_FAR + (0,):
-                    to_other_core(oz).start()
+                for oz, r in RING:
+                    square_to(oz, r).start()
             lhs = stacked(line)
             for n, r in enumerate(FAR_FIRST):
                 p = lax.rem(zp + r, PAIRS)
@@ -377,26 +389,24 @@
                 if dx != NEAR_FIRST[-1]:
                     col_a[n] = part
                 else:
-                    bak_p[2 * p, :OUTS] = part[:, :PIECE]
-                    bak_p[2 * p + 1, :OUTS] = part[:, PIECE:]
+                    bak_p[2 * p] = part[:, :PIECE]
+                    bak_p[2 * p + 1] = part[:, PIECE:]
                     scatter_z(bak_p, bak_r, bak_ss, bak_rs, r)
         sent_plane(fwd_f, fwf_ss, fwf_rs)
-        total = z_sum(bak_p, bak_r, bak_ss, bak_rs)
-        square = total[OUTS:]
-        for oz in range(Z):
-            to_other_core(oz).wait_recv()
-            square = square + sq_r[step, oz]
-        square = jnp.sum(jnp.sum(square, axis=1, keepdims=True), axis=0, keepdims=True)
+        for oz, r in reversed(RING):
+            square_to(oz, r).wait_recv()
+            square = square + sq_r[step, oz * 2 + r]
+        square = jnp.sum(square, axis=1, keepdims=True)
         scale = step_size / jnp.sqrt(square / (CENT * 2 * CHIPS * OUT) + epsilon)
-        a_f[z] = a_f[z] - scale * total[:OUTS]
+        a_f[z] = a_f[z] - scale * z_sum(bak_p, bak_r, bak_ss, bak_rs)
 
         @pl.when(step < STEPS - 1)
         def _():
             gather_z(a_f, af_ss, af_rs)
 
         sent_z(bak_p, bak_ss, bak_rs)
-        for oz in range(Z):
-            to_other_core(oz).wait_send()
+        for oz, r in RING:
+            square_to(oz, r).wait_send()
 
         @pl.when(step < STEPS - 1)
         def _():
@@ -475,9 +485,13 @@
         V((8, ROWS), f32),
         V((2, CENT, ROWS), bf16),
         V((2, CENT, ROWS), bf16),
+        V((2, ROWS, CENT), bf16),
+        V((2, ROWS, CENT), bf16),
         V((2, PROWS, CENT), f32),
         V((2, PROWS, CENT), bf16),
         V((2, PROWS, CENT), bf16),
+        V((2, CENT, PROWS), bf16),
+        V((2, CENT, PROWS), bf16),
         V((X, OUTS, RS_ROWS), f32),
         V((X, OUTS, RS_ROWS), f32),
         V((X, OUTS, RS_ROWS), f32),
@@ -492,11 +506,11 @@
         V((CHIPS, 8, RS_PROWS), f32),
         V((CHIPS, 8, RS_PROWS), f32),
         V((CHIPS, 8, RS_PROWS), f32),
-        V((Z, OUTS + 8, PIECE), f32),
-        V((Z, OUTS + 8, PIECE), f32),
-        V((Z, OUTS, PIECE), f32),
-        V((STEPS, 8, 128), f32),
-        V((STEPS, Z, 8, 128), f32),
+        V((Z, OUTS, PIECE), f32),
+        V((Z, OUTS, PIECE), f32),
+        V((Z, OUTS, PIECE), f32),
+        V((STEPS, 1, 128), f32),
+        V((STEPS, 2 * Z, 1, 128), f32),
         V((Z, OUTS, PIECE), f32),
         dma((5,)),
         dma((9,)),
@@ -506,7 +520,7 @@
     ]
     for count in (CHIPS, CHIPS, Z, Z, CHIPS, CHIPS, Z, Z):
         scratch += [dma((count,)), dma((count,))]
-    scratch += [dma((STEPS, Z)), dma((STEPS, Z)), dma((Z,)), dma((2 * Z,))]
+    scratch += [dma((STEPS, 2 * Z)), dma((STEPS, 2 * Z)), dma((Z,)), dma((2 * Z,))]
     out = pl.pallas_call(
         kernel,
         out_shape=pltpu.VMEM((OUT, CENT), f32),

time: 105 us -> 104 us (level)
    pallas_call x1, Pallas kernels: 104 us -> 103 us  [body(): pl.pallas_call(kernel, out_shape=pltpu.VMEM((OUT, CENT), f32), in_specs=[...]
where the time goes in v3:
time: 104 us
  Pallas kernels  103 us (99%)
    pallas_call x1, Pallas kernels, body(): pl.pallas_call(kernel, out_shape=pltpu.VMEM((OUT, CENT), f32), in_specs=[...  103 us

profile of v3, /device:TPU:1, one launch (start us, length us, event | category | flops | bytes accessed | tf_op | source)
XLA Modules:
  0.0 103.9 jit_solution(8327628623653571391)
XLA Ops:
  0.0 103.2 %falkon.1 = f32[64,512]{1,0:T(8,128)S(1)} custom-call(f32[1024,128]{1,0:T(8,128)} %feat_hbm.1, f32[512,128]{1,0:T(8,128)} %cent_hbm.1, s32[64,1024]{1,0:T(8,128)} %bitcast.4, f32[64,512]{1,0:T(8,128)} %bitcast.5, f32[2048,512]{1,0:T(8,128)} %prec_hbm.1), custom_call_target="tpu_custom_call" | custom-call | tf_op jit(solution)/shard_map/falkon/pallas_call | solution.py:524
  103.2 0.7 copy.7

commit v4 on v3

--- a/solution.py
+++ b/solution.py
@@ -194,6 +194,9 @@
 
     def line_of(pieces, rg):
         return jnp.concatenate([pieces[og * X + rg] for og in range(GROUPS)], axis=0)
+
+    def half_of(pieces, h):
+        return jnp.concatenate([pieces[h * (Z // 2) + i] for i in range(Z // 2)], axis=1)
 
     def pair_of(pieces, p):
         return jnp.concatenate([pieces[2 * p], pieces[2 * p + 1]], axis=1)
@@ -339,20 +342,13 @@
 
         for r in NEAR_FIRST:
             arrived_pair(gra_f, grf_ss, grf_rs, r)
-            p = lax.rem(zp + r, PAIRS)
-            h, at = pair_at(p)
-            lhs = stacked(pair_of(gra_f, p))
-            for n, dx in enumerate(FAR_FIRST):
-                rg, rows = row_block(dx, RS_PROWS)
-                part = product(lhs, pt_hi[h, at, rows], pt_lo[h, at, rows], 0)
-                if r != NEAR_FIRST[0]:
-                    part = fwd_a[n] + part
-                if r != NEAR_FIRST[-1]:
-                    fwd_a[n] = part
-                else:
-                    for og in range(GROUPS):
-                        fwd_p[og * X + rg] = part[og * 8 : og * 8 + 8]
-                    scatter_plane(fwd_p, fwd_r, fwd_ss, fwd_rs, dx)
+        halves = [stacked(half_of(gra_f, h)) for h in range(2)]
+        for dx in FAR_FIRST:
+            rg, rows = row_block(dx, RS_PROWS)
+            part = sum(product(halves[h], pt_hi[h, :, rows], pt_lo[h, :, rows], 0) for h in range(2))
+            for og in range(GROUPS):
+                fwd_p[og * X + rg] = part[og * 8 : og * 8 + 8]
+            scatter_plane(fwd_p, fwd_r, fwd_ss, fwd_rs, dx)
         sent_z(gra_f, grf_ss, grf_rs)
         fwd_f[j] = plane_sum(fwd_p, fwd_r, fwd_ss, fwd_rs)
         gather_plane(fwd_f, fwf_ss, fwf_rs)
@@ -412,18 +408,10 @@
         def _():
             for r in NEAR_FIRST:
                 arrived_pair(a_f, af_ss, af_rs, r)
-                p = lax.rem(zp + r, PAIRS)
-                h, at = pair_at(p)
-                lhs = stacked(pair_of(a_f, p))
-                for n, dx in enumerate(FAR_FIRST):
-                    rg, rows = row_block(dx, RS_ROWS)
-                    part = product(lhs, k_hi[h, at, rows], k_lo[h, at, rows], 0)
-                    if r != NEAR_FIRST[0]:
-                        part = log_a[n] + part
-                    if r != NEAR_FIRST[-1]:
-                        log_a[n] = part
-                    else:
-                        send_logits(dx, part)
+            halves = [stacked(half_of(a_f, h)) for h in range(2)]
+            for dx in FAR_FIRST:
+                rg, rows = row_block(dx, RS_ROWS)
+                send_logits(dx, sum(product(halves[h], k_hi[h, :, rows], k_lo[h, :, rows], 0) for h in range(2)))
             sent_z(a_f, af_ss, af_rs)
 
     holder = z // (Z // 2)

time: 104 us -> 104 us (level)
  no operation moved by 1% of the time
where the time goes in v4:
time: 104 us
  Pallas kernels  103 us (99%)
    pallas_call x1, Pallas kernels, body(): pl.pallas_call(kernel, out_shape=pltpu.VMEM((OUT, CENT), f32), in_specs=[...  103 us

profile of v4, /device:TPU:1, one launch (start us, length us, event | category | flops | bytes accessed | tf_op | source)
XLA Modules:
  0.0 103.8 jit_solution(9068608367674966928)
XLA Ops:
  0.0 103.1 %falkon.1 = f32[64,512]{1,0:T(8,128)S(1)} custom-call(f32[1024,128]{1,0:T(8,128)} %feat_hbm.1, f32[512,128]{1,0:T(8,128)} %cent_hbm.1, s32[64,1024]{1,0:T(8,128)} %bitcast.4, f32[64,512]{1,0:T(8,128)} %bitcast.5, f32[2048,512]{1,0:T(8,128)} %prec_hbm.1), custom_call_target="tpu_custom_call" | custom-call | tf_op jit(solution)/shard_map/falkon/pallas_call | solution.py:512
  103.1 0.7 copy.7
